TPU v7x, 32 devices: a whole 2x2x4 slice. The times are simulated.
32 devices in a mesh: row: 8 (over z, x), col: 2 (over y), depth: 2 (over core).
Axes of the slice: x: 2, y: 2, z: 4, core: 2. Of those that a mesh axis runs over, the one named last changes fastest.
Arguments:
- tokens: bfloat16 [1024, 5376], P('row', 'depth'), may hold values from -6 to 6
- gate_weight: bfloat16 [9216, 5376], P(('col', 'row'), 'depth'), may hold values from -0.078125 to 0.078125
- up_weight: bfloat16 [9216, 5376], P(('col', 'row'), 'depth'), may hold values from -0.078125 to 0.078125
- down_weight: bfloat16 [9216, 5376], P(('col', 'depth'), 'row'), may hold values from -0.09375 to 0.09375
Outputs:
- output: bfloat16 [1024, 5376], P('row', ('col', 'depth'))
All inputs are finite; a program needn't handle non-finite values.
Results may differ from a plain program's by a relative error of at most 0.0049.
Values may be sent and summed in bfloat16 or wider, within the bound.
A program may use at most 128 MiB of HBM per device.

v0:
```python
import jax
import jax.numpy as jnp
from jax import lax
from jax.sharding import PartitionSpec as P


def local(tokens, gate_weight, up_weight, down_weight):
    paired = jnp.stack([gate_weight, up_weight])
    every_token = jnp.einsum(
        "td,gfd->gtf",
        lax.all_gather(tokens, "row", axis=0, tiled=True),
        paired,
        preferred_element_type=jnp.float32,
    )
    partial_sums = lax.all_to_all(every_token, "row", split_axis=1, concat_axis=2, tiled=True)
    share_width = partial_sums.shape[2] // lax.axis_size("depth")
    summed = lax.psum(partial_sums, "depth")
    shares = lax.dynamic_slice_in_dim(summed, lax.axis_index("depth") * share_width, share_width, 2)
    hidden = (jax.nn.silu(shares[0]) * shares[1]).astype(jnp.bfloat16)
    down_terms = jnp.dot(
        hidden,
        lax.all_gather(down_weight, "row", axis=1, tiled=True),
        preferred_element_type=jnp.float32,
    )
    return lax.psum_scatter(down_terms, ("col", "depth"), scatter_dimension=1, tiled=True).astype(
        jnp.bfloat16
    )


def solution(mesh):
    in_specs = (
        P("row", "depth"),
        P(("col", "row"), "depth"),
        P(("col", "row"), "depth"),
        P(("col", "depth"), "row"),
    )
    out_specs = P("row", ("col", "depth"))
    return jax.shard_map(local, mesh=mesh, in_specs=in_specs, out_specs=out_specs, check_vma=False)
```

profile of v0, /device:TPU:0, one launch (start us, length us, event | category | flops | bytes accessed | tf_op | source)
XLA Modules:
  0.0 810.8 jit_solution(2922904456121408201)
XLA Ops:
  6.5 0.0 all-gather.3.cloned.1.call-start
  6.5 0.7 all-gather.3.cloned.1.call-update
  7.3 0.0 all-reduce.2.cloned.1.call-start
  7.3 94.1 %all-gather.3.cloned.1.call-done = bf16[1024,2688]{1,0:T(8,128)(2,1)} async-done(((bf16[128,2688]{1,0:T(8,128)(2,1)}), bf16[1024,2688]{1,0:T(8,128)(2,1)}) %all-gather.3.cloned.1.call-update) | async-done | bytes 5505040 | tf_op jit(solution)/shard_map/all_gather | solution.py:11
  101.4 12.0 %fusion.5 = f32[2,1024,576]{1,2,0:T(8,128)} fusion(bf16[1024,2688]{1,0:T(8,128)(2,1)} %all-gather.3.cloned.1.call-done, bf16[1,576,2688]{2,1,0:T(8,128)(2,1)} %bitcast.29, bf16[1,576,2688]{2,1,0:T(8,128)(2,1)} %bitcast.30), kind=kOutput, calls=%fused_computation.5 | convolution fusion | flops 6344884224 | bytes 16416768 | tf_op jit(solution)/shard_map/td,gfd->gtf/dot_general | solution.py:9
  113.4 8.8 %copy.7 = f32[2,1024,576]{2,0,1:T(2,128)} copy(f32[2,1024,576]{1,2,0:T(8,128)} %fusion.5) | data formatting | bytes 9437184 | tf_op jit(solution)/shard_map/td,gfd->gtf/transpose | solution.py:9
  122.1 118.9 %all_to_all.18 = f32[2,1024,576]{2,0,1:T(2,128)} all-to-all(f32[2,1024,576]{2,0,1:T(2,128)} %copy.7), channel_id=1, replica_groups=mesh['row'=8,'col'=2,'depth'=2] {'row'}, dimensions={1} | all-to-all | bytes 9437184 | tf_op jit(solution)/shard_map/all_to_all | solution.py:15
  241.1 8.7 %copy.11 = f32[2,8,128,576]{2,3,1,0:T(8,128)} copy(f32[2,8,128,576]{3,0,2,1:T(2,128)} %bitcast.27) | data formatting | bytes 9437184 | tf_op jit(solution)/shard_map/all_to_all | solution.py:15
  249.7 0.0 all-reduce.2.cloned.1.call-update
  249.8 0.0 all-gather.5.cloned.1.call-start
  249.8 0.7 all-gather.5.cloned.1.call-update
  250.5 0.0 reduce-scatter.2.cloned.1.call-start
  250.6 27.2 %all-reduce.2.cloned.1.call-done = f32[2,128,4608]{1,2,0:T(8,128)} async-done(((f32[2,128,4608]{1,2,0:T(8,128)}), f32[2,128,4608]{1,2,0:T(8,128)}) %all-reduce.2.cloned.1.call-update) | async-done | bytes 4718608 | tf_op jit(solution)/shard_map/psum | solution.py:17
  277.8 475.7 %all-gather.5.cloned.1.call-done = bf16[2304,5376]{0,1:T(8,128)(2,1)} async-done(((bf16[2304,672]{0,1:T(8,128)(2,1)}), bf16[2304,5376]{0,1:T(8,128)(2,1)}) %all-gather.5.cloned.1.call-update) | async-done | bytes 24772624 | tf_op jit(solution)/shard_map/all_gather | solution.py:22
  753.5 13.3 %fusion.12 = f32[128,5376]{0,1:T(8,128)} fusion(bf16[2304,5376]{0,1:T(8,128)(2,1)} %all-gather.5.cloned.1.call-done, f32[2,128,4608]{1,2,0:T(8,128)} %all-reduce.2.cloned.1.call-done, s32[]{:T(128)S(6)} %add.13, s32[]{:T(128)S(6)} %select_n.3), kind=kOutput, calls=%fused_computation.10 | convolution fusion | flops 3172663296 | bytes 29884424 | tf_op jit(solution)/shard_map/dot_general | solution.py:20
  766.9 0.0 reduce-scatter.2.cloned.1.call-update
  766.9 35.5 %reduce-scatter.2.cloned.1.call-done = f32[128,1344]{0,1:T(8,128)} async-done(((f32[128,5376]{0,1:T(8,128)}), f32[128,1344]{0,1:T(8,128)}) %reduce-scatter.2.cloned.1.call-update) | async-done | bytes 688144 | tf_op jit(solution)/shard_map/reduce_scatter | solution.py:25
  802.4 1.9 convert_element_type.7
Async XLA Ops:
  6.5 94.9 %all-gather.3.cloned.1.call-start = ((), (), s32[]{:S(2)}) async-start(), calls=%async_computation.2 | async-start | bytes 6193152 | tf_op jit(solution)/shard_map/all_gather | solution.py:11
  7.3 270.5 %all-reduce.2.cloned.1.call-start = ((), (), s32[]{:S(2)}) async-start(), calls=%async_computation.3 | async-start | bytes 9437184 | tf_op jit(solution)/shard_map/psum | solution.py:17
  249.8 503.8 %all-gather.5.cloned.1.call-start = ((), (), s32[]{:S(2)}) async-start(), calls=%async_computation.4 | async-start | bytes 27869184 | tf_op jit(solution)/shard_map/all_gather | solution.py:22
  250.5 551.9 %reduce-scatter.2.cloned.1.call-start = ((), (), s32[]{:S(2)}) async-start(), calls=%async_computation.5 | async-start | bytes 3440640 | tf_op jit(solution)/shard_map/reduce_scatter | solution.py:25
Sparse Core Ops, SparseCore 0:
  9.5 91.8 all-gather.2
  249.9 27.8 all-reduce.1
  279.3 474.1 all-gather.4
  767.0 35.2 reduce-scatter.1
where the time goes:
time: 811 us
  waiting for transfers between devices  634 us (78%)
  blocking collectives  119 us (15%)
  matrix products  25.3 us (3%)
  local copies, waits for them, and re-layouts  17.5 us (2%)
  between operations  13.1 us (2%)
    all_gather x1, waiting for transfers between devices, local(): lax.all_gather(down_weight, 'row', axis=1, tiled=True)  476 us
    all_to_all x1, blocking collectives, local(): lax.all_to_all(every_token, 'row', split_axis=1, concat_axis=2, tiled=True)  119 us
    all_gather x1, waiting for transfers between devices, local(): lax.all_gather(tokens, 'row', axis=0, tiled=True)  94.1 us
    reduce_scatter x1, waiting for transfers between devices, local(): lax.psum_scatter(down_terms, ('col', 'depth'), scatter_dimension=1, tiled...  35.5 us
    psum x1, waiting for transfers between devices, local(): summed = lax.psum(partial_sums, 'depth')  27.2 us
  transfers between devices with their start and end apart: 4, of which 4 were waited for; matrix products, arithmetic and copies ran while one was open for 0% of the time, Pallas kernels for 0%

commit v1 on v0

--- a/solution.py
+++ b/solution.py
@@ -19,7 +19,7 @@
     hidden = (jax.nn.silu(shares[0]) * shares[1]).astype(jnp.bfloat16)
     down_terms = jnp.dot(
         hidden,
-        lax.all_gather(down_weight, "row", axis=1, tiled=True),
+        jnp.concatenate(lax.all_gather(down_weight, "row"), axis=1),
         preferred_element_type=jnp.float32,
     )
     return lax.psum_scatter(down_terms, ("col", "depth"), scatter_dimension=1, tiled=True).astype(

time: 811 us -> 721 us (0.89)
  waiting for transfers between devices: 634 us -> 450 us
  blocking collectives: 119 us -> 183 us
  local copies, waits for them, and re-layouts: 17.5 us -> 46.2 us
    all_gather x1, waiting for transfers between devices: 476 us -> 316 us  [local(): lax.all_gather(down_weight, 'row')]
    all_to_all x1, blocking collectives: 119 us -> 183 us  [local(): lax.all_to_all(every_token, 'row', split_axis=1, concat_axis=2, tiled=True)]
    psum x1, waiting for transfers between devices: 27.2 us -> 2.6 us  [local(): summed = lax.psum(partial_sums, 'depth')]
    unnamed x0 -> x1, local copies, waits for them, and re-layouts: none -> 16.8 us
    reshape x0 -> x1, local copies, waits for them, and re-layouts: none -> 12.1 us  [local(): jnp.concatenate(lax.all_gather(down_weight, 'row'), axis=1)]
  transfers between devices with their start and end apart: 4 -> 4, of which waited for: 4 -> 4; matrix products, arithmetic and copies ran while one was open for 0% -> 8% of each run, Pallas kernels for 0% -> 0%
where the time goes in v1:
time: 721 us; the launch traced here: 720 us
  waiting for transfers between devices  450 us (62%)
  blocking collectives  183 us (25%)
  local copies, waits for them, and re-layouts  46.2 us (6%)
  matrix products  25.3 us (4%)
  between operations  13.1 us (2%)
    all_gather x1, waiting for transfers between devices, local(): lax.all_gather(down_weight, 'row')  316 us
    all_to_all x1, blocking collectives, local(): lax.all_to_all(every_token, 'row', split_axis=1, concat_axis=2, tiled=True)  183 us
    all_gather x1, waiting for transfers between devices, local(): lax.all_gather(tokens, 'row', axis=0, tiled=True)  93.3 us
    reduce_scatter x1, waiting for transfers between devices, local(): lax.psum_scatter(down_terms, ('col', 'depth'), scatter_dimension=1, tiled...  36.7 us
    unnamed x1, local copies, waits for them, and re-layouts  16.8 us
  transfers between devices with their start and end apart: 4, of which 4 were waited for; matrix products, arithmetic and copies ran while one was open for 8% of the time, Pallas kernels for 0%

profile of v1, /device:TPU:0, one launch (start us, length us, event | category | flops | bytes accessed | tf_op | source)
XLA Modules:
  0.0 720.1 jit_solution(5834530495781599081)
XLA Ops:
  6.5 0.0 all-gather.4.cloned.1.call-start
  6.5 0.7 all-gather.4.cloned.1.call-update
  7.3 0.0 all-gather.6.cloned.1.call-start
  7.3 0.7 all-gather.6.cloned.1.call-update
  8.0 0.0 all-reduce.2.cloned.1.call-start
  8.1 93.3 %all-gather.4.cloned.1.call-done = bf16[1024,2688]{1,0:T(8,128)(2,1)} async-done(((bf16[128,2688]{1,0:T(8,128)(2,1)}), bf16[1024,2688]{1,0:T(8,128)(2,1)}) %all-gather.4.cloned.1.call-update) | async-done | bytes 5505040 | tf_op jit(solution)/shard_map/all_gather | solution.py:11
  101.4 12.0 %fusion.5 = f32[2,1024,576]{1,2,0:T(8,128)} fusion(bf16[1024,2688]{1,0:T(8,128)(2,1)} %all-gather.4.cloned.1.call-done, bf16[1,576,2688]{2,1,0:T(8,128)(2,1)} %bitcast.30, bf16[1,576,2688]{2,1,0:T(8,128)(2,1)} %bitcast.31), kind=kOutput, calls=%fused_computation.5 | convolution fusion | flops 6344884224 | bytes 16416768 | tf_op jit(solution)/shard_map/td,gfd->gtf/dot_general | solution.py:9
  113.4 8.7 %copy.10 = f32[2,1024,576]{2,0,1:T(2,128)} copy(f32[2,1024,576]{1,2,0:T(8,128)} %fusion.5) | data formatting | bytes 9437184 | tf_op jit(solution)/shard_map/td,gfd->gtf/transpose | solution.py:9
  122.1 183.3 %all_to_all.18 = f32[2,1024,576]{2,0,1:T(2,128)} all-to-all(f32[2,1024,576]{2,0,1:T(2,128)} %copy.10), channel_id=1, replica_groups=mesh['row'=8,'col'=2,'depth'=2] {'row'}, dimensions={1} | all-to-all | bytes 9437184 | tf_op jit(solution)/shard_map/all_to_all | solution.py:15
  305.4 8.7 %copy.15 = f32[2,8,128,576]{2,3,1,0:T(8,128)} copy(f32[2,8,128,576]{3,0,2,1:T(2,128)} %bitcast.28) | data formatting | bytes 9437184 | tf_op jit(solution)/shard_map/all_to_all | solution.py:15
  314.1 0.0 all-reduce.2.cloned.1.call-update
  314.1 0.0 reduce-scatter.2.cloned.1.call-start
  314.2 316.1 %all-gather.6.cloned.1.call-done = bf16[18432,672]{0,1:T(8,128)(2,1)} async-done(((bf16[2304,672]{0,1:T(8,128)(2,1)}), bf16[18432,672]{0,1:T(8,128)(2,1)}) %all-gather.6.cloned.1.call-update) | async-done | bytes 24772624 | tf_op jit(solution)/shard_map/all_gather | solution.py:22
  630.3 16.8 %copy.16 = bf16[84,8,8,2304]{3,2,1,0:T(8,128)(2,1)S(1)} copy(bf16[84,8,8,2304]{3,1,2,0:T(8,128)(2,1)} %bitcast.26) | data formatting | bytes 49545216
  647.0 12.1 %copy.13 = bf16[2304,8,672]{0,2,1:T(8,128)(2,1)} copy(bf16[2304,8,672]{0,1,2:T(8,128)(2,1)S(1)} %bitcast.25) | data formatting | bytes 49545216 | tf_op jit(solution)/shard_map/reshape | solution.py:22
  659.1 2.6 all-reduce.2.cloned.1.call-done
  661.7 13.3 %fusion.11 = f32[128,5376]{0,1:T(8,128)} fusion(bf16[2304,5376]{0,1:T(8,128)(2,1)} %bitcast.27, f32[2,128,4608]{1,2,0:T(8,128)} %all-reduce.2.cloned.1.call-done, s32[]{:T(128)S(6)} %add.14, s32[]{:T(128)S(6)} %select_n.3), kind=kOutput, calls=%fused_computation.8 | convolution fusion | flops 3172663296 | bytes 29884424 | tf_op jit(solution)/shard_map/dot_general | solution.py:20
  675.0 0.0 reduce-scatter.2.cloned.1.call-update
  675.1 36.7 %reduce-scatter.2.cloned.1.call-done = f32[128,1344]{0,1:T(8,128)} async-done(((f32[128,5376]{0,1:T(8,128)}), f32[128,1344]{0,1:T(8,128)}) %reduce-scatter.2.cloned.1.call-update) | async-done | bytes 688144 | tf_op jit(solution)/shard_map/reduce_scatter | solution.py:25
  711.7 1.9 convert_element_type.11
Async XLA Ops:
  6.5 94.9 %all-gather.4.cloned.1.call-start = ((), (), s32[]{:S(2)}) async-start(), calls=%async_computation.2 | async-start | bytes 6193152 | tf_op jit(solution)/shard_map/all_gather | solution.py:11
  7.3 623.0 %all-gather.6.cloned.1.call-start = ((), (), s32[]{:S(2)}) async-start(), calls=%async_computation.5 | async-start | bytes 27869184 | tf_op jit(solution)/shard_map/all_gather | solution.py:22
  8.0 653.7 %all-reduce.2.cloned.1.call-start = ((), (), s32[]{:S(2)}) async-start(), calls=%async_computation.3 | async-start | bytes 9437184 | tf_op jit(solution)/shard_map/psum | solution.py:17
  314.1 397.6 %reduce-scatter.2.cloned.1.call-start = ((), (), s32[]{:S(2)}) async-start(), calls=%async_computation.4 | async-start | bytes 3440640 | tf_op jit(solution)/shard_map/reduce_scatter | solution.py:25
Sparse Core Ops, SparseCore 0:
  9.5 91.8 all-gather.3
  102.9 527.2 all-gather.5
  632.8 28.8 all-reduce.1
  675.2 36.5 reduce-scatter.1
